TPU v7x, 32 devices: a whole 2x2x4 slice. The times are simulated.
32 devices in a mesh: node: 8 (over z, x), rep: 4 (over y, core).
Axes of the slice: x: 2, y: 2, z: 4, core: 2. Of those that a mesh axis runs over, the one named last changes fastest.
Arguments:
- features: bfloat16 [163840, 256], P('node'), may hold values from -6 to 6
- w_in: bfloat16 [256, 256], replicated, may hold values from -0.375 to 0.375
- w_out: bfloat16 [256, 256], replicated, may hold values from -0.375 to 0.375
- pos_src: int32 [8, 4, 8, 2], P('node', 'rep'), may hold values from 0 to 159
- pos_dst: int32 [8, 4, 8, 2], P('node', 'rep'), may hold values from 0 to 159
- counts: int32 [8, 4, 8], P('node', 'rep'), may hold values from 1 to 2, as said below
- neg_blocks: int32 [8, 2], P('node'), may hold values from 0 to 159
- neg_pick: int32 [8, 4, 8, 2], P('node', 'rep'), may hold values from 0 to 15
Outputs:
- pos_scores: float32 [8, 4, 8, 2, 128], P('node', 'rep')
- neg_term: float32 [8, 4, 8, 2, 128], P('node', 'rep')
- loss: float32 [], replicated
Inputs may be any that keep to these rules, and one draw needn't show every extreme that they name: `counts`: each entry is at most 2; in every draw one owner receives 2 live slots from every device.
All inputs are finite; a program needn't handle non-finite values.
Results may differ from a plain program's by a relative error of at most 0.0027.
Values may be sent and summed in bfloat16 or wider, within the bound.
A program may use at most 192 MiB of HBM per device.

v0:
```python
import jax
import jax.numpy as jnp
from jax import lax
from jax.sharding import PartitionSpec as P

BLK = 128


def encode(rows_in, w_in, w_out):
    hidden = jax.nn.silu(jnp.dot(rows_in, w_in, preferred_element_type=jnp.float32)).astype(
        jnp.bfloat16
    )
    return jnp.dot(hidden, w_out, preferred_element_type=jnp.float32).astype(jnp.bfloat16)


def shards(features, w_in, w_out, pos_src, pos_dst, counts, neg_blocks, neg_pick):
    rows, width = features.shape
    owners = pos_dst.shape[2]
    slots = pos_dst.shape[3]
    embed = encode(features, w_in, w_out)
    blocks = embed.reshape(rows // BLK, BLK, width)
    asked_ids = pos_dst.reshape(owners, slots)
    reply = jnp.take(
        blocks, lax.all_to_all(asked_ids, "node", split_axis=0, concat_axis=0, tiled=True), axis=0
    )
    fetched = lax.all_to_all(reply, "node", split_axis=0, concat_axis=0, tiled=True)
    offered = jnp.take(blocks, neg_blocks.reshape(-1), axis=0)
    pool = lax.all_gather(offered, "node", axis=0, tiled=True)
    source = jnp.take(blocks, pos_src.reshape(-1), axis=0).reshape(owners, slots, BLK, width)
    cand = jnp.take(pool, neg_pick.reshape(-1), axis=0).reshape(owners, slots, BLK, width)
    scale = 1.0 / width**0.5
    raw_pos = (
        jnp.einsum("ocbd,ocbd->ocb", source, fetched, preferred_element_type=jnp.float32) * scale
    )
    scores = jnp.einsum("ocbd,ocsd->ocbs", source, cand, preferred_element_type=jnp.float32) * scale
    live = jnp.arange(slots, dtype=jnp.int32)[None, :] < counts.reshape(owners, 1)
    livex = live[..., None]
    pos_out = jnp.where(livex, raw_pos, 0.0)
    neg_out = jnp.where(livex, jnp.mean(jax.nn.softplus(scores), axis=-1), 0.0)
    pos_loss = jnp.sum(jnp.where(livex, jax.nn.softplus(-raw_pos), 0.0))
    totals = lax.psum(
        (pos_loss, jnp.sum(neg_out), jnp.sum(counts).astype(jnp.float32)), ("node", "rep")
    )
    loss = (totals[0] + totals[1]) / (BLK * totals[2])
    return (
        pos_out.reshape(1, 1, owners, slots, BLK),
        neg_out.reshape(1, 1, owners, slots, BLK),
        loss,
    )


def solution(mesh):
    return jax.shard_map(
        shards,
        mesh=mesh,
        in_specs=(
            P("node", None),
            P(),
            P(),
            P("node", "rep", None, None),
            P("node", "rep", None, None),
            P("node", "rep", None),
            P("node", None),
            P("node", "rep", None, None),
        ),
        out_specs=(P("node", "rep", None, None, None), P("node", "rep", None, None, None), P()),
        check_vma=False,
    )
```

profile of v0, /device:TPU:0, one launch (start us, length us, event | category | flops | bytes accessed | tf_op | source)
XLA Modules:
  0.0 137.5 jit_solution(16845520026060009428)
XLA Ops:
  7.2 1.4 %copy.25 = s32[8,1,2]{2,1,0:T(1,128)} copy(s32[8,1,2]{0,2,1:T(2,128)} %bitcast.44) | data formatting | bytes 128 | tf_op jit(solution)/shard_map/all_to_all | solution.py:24
  8.6 7.3 %all-to-all-start = ((s32[8,1,2]{2,1,0:T(1,128)}), s32[8,1,2]{2,1,0:T(1,128)S(1)}, u32[]{:S(2)}, u32[]{:S(2)}) async-start(s32[8,1,2]{2,1,0:T(1,128)} %copy.25), calls=%async_computation | async-start | bytes 8192 | tf_op jit(solution)/shard_map/all_to_all | solution.py:24
  15.9 0.7 fusion.8
  16.5 0.7 compare_and_fusion
  17.3 10.9 %convolution_convert_fusion = bf16[20480,256]{1,0:T(8,128)(2,1)} fusion(bf16[256,256]{1,0:T(8,128)(2,1)S(1)} %copy-done, bf16[20480,256]{1,0:T(8,128)(2,1)} %param.8, bf16[256,256]{1,0:T(8,128)(2,1)} %param.9), kind=kOutput, calls=%fused_computation.4 | convolution fusion | flops 5400166400 | bytes 21233664 | tf_op jit(solution)/shard_map/dot_general | solution.py:13
  28.2 4.5 %gather_fusion.2 = bf16[2,128,256]{2,1,0:T(8,128)(2,1)S(1)} fusion(bf16[160,128,256]{2,1,0:T(8,128)(2,1)} %bitcast.41, s32[1024]{0:T(1024)S(1)} %pad_clamp_fusion.1), kind=kCustom, calls=%fused_computation.2 | custom fusion | bytes 262152 | tf_op jit(solution)/shard_map/jit(_take)/gather | solution.py:27
  32.7 0.7 broadcast_select_fusion.3
  33.5 0.6 reduce_sum.39
  34.8 0.1 copy.24
  35.0 0.1 copy.27
  35.2 4.6 %gather_fusion.1 = bf16[16,128,256]{2,1,0:T(8,128)(2,1)S(1)} fusion(bf16[160,128,256]{2,1,0:T(8,128)(2,1)} %bitcast.42, s32[1024]{0:T(1024)S(1)} %pad_clamp_fusion.2), kind=kCustom, calls=%fused_computation.1 | custom fusion | bytes 2097216 | tf_op jit(solution)/shard_map/jit(_take)/gather | solution.py:23
  39.8 1.1 broadcast_select_fusion
  41.0 6.0 %all-to-all-start.1 = ((bf16[8,2,128,256]{3,2,1,0:T(8,128)(2,1)}), bf16[8,2,128,256]{3,2,1,0:T(8,128)(2,1)S(1)}, u32[]{:S(2)}, u32[]{:S(2)}) async-start(bf16[8,2,128,256]{3,2,1,0:T(8,128)(2,1)} %broadcast_select_fusion), calls=%async_computation.1 | async-start | bytes 2097152 | tf_op jit(solution)/shard_map/all_to_all | solution.py:26
  46.9 0.1 copy.23
  47.1 0.1 copy.30
  47.4 4.6 %gather_fusion = bf16[16,128,256]{2,1,0:T(8,128)(2,1)S(1)} fusion(bf16[160,128,256]{2,1,0:T(8,128)(2,1)} %bitcast.43, s32[1024]{0:T(1024)S(1)} %pad_clamp_fusion.3), kind=kCustom, calls=%fused_computation | custom fusion | bytes 2097216 | tf_op jit(solution)/shard_map/jit(_take)/gather | solution.py:29
  52.1 30.7 %all-gather.2.cloned.1.call-done = bf16[16,128,256]{2,1,0:T(8,128)(2,1)} async-done(((bf16[2,128,256]{2,1,0:T(8,128)(2,1)}), bf16[16,128,256]{2,1,0:T(8,128)(2,1)}) %all-gather.2.cloned.1.call-update) | async-done | bytes 1048592 | tf_op jit(solution)/shard_map/all_gather | solution.py:28
  82.8 1.8 %gather_fusion.3 = bf16[16,128,256]{2,1,0:T(8,128)(2,1)S(1)} fusion(bf16[16,128,256]{2,1,0:T(8,128)(2,1)} %all-gather.2.cloned.1.call-done, s32[1024]{0:T(1024)S(1)} %pad_clamp_fusion), kind=kCustom, calls=%fused_computation.3 | custom fusion | bytes 2097216 | tf_op jit(solution)/shard_map/jit(_take)/gather | solution.py:30
  84.7 0.5 fusion.4
  85.2 0.6 select_reduce_fusion
  85.9 0.5 fusion
  86.4 1.3 select_reduce_fusion.1
  89.0 0.7 bitcast_select_fusion
  89.7 38.6 %all-reduce = (f32[]{:T(128)}, f32[]{:T(128)}) all-reduce(f32[]{:T(128)S(6)} %add.94, f32[]{:T(128)S(6)} %convert_element_type.11), channel_id=1, replica_groups=mesh['node'=8,'rep'=4] {'node','rep'}, use_global_device_ids=true, to_apply=%region_2.3 | all-reduce | flops 2 | bytes 16 | tf_op jit(solution)/shard_map/psum | solution.py:41
  (29 shorter events, 0.7 us)
Async XLA Ops:
  7.2 10.1 %copy-start = (bf16[256,256]{1,0:T(8,128)(2,1)S(1)}, bf16[256,256]{1,0:T(8,128)(2,1)}, u32[]{:S(2)}) copy-start(bf16[256,256]{1,0:T(8,128)(2,1)} %param.10) | copy-start | bytes 393220
  8.6 26.3 %all-to-all-start = ((s32[8,1,2]{2,1,0:T(1,128)}), s32[8,1,2]{2,1,0:T(1,128)S(1)}, u32[]{:S(2)}, u32[]{:S(2)}) async-start(s32[8,1,2]{2,1,0:T(1,128)} %copy.25), calls=%async_computation | async-start | bytes 8192 | tf_op jit(solution)/shard_map/all_to_all | solution.py:24
  15.8 67.0 %all-gather.2.cloned.1.call-start = ((), (), s32[]{:S(2)}) async-start(), calls=%async_computation.2 | async-start | bytes 1179648 | tf_op jit(solution)/shard_map/all_gather | solution.py:28
  17.2 16.3 %copy-start.3 = (s32[1,1,8]{2,1,0:T(1,128)S(1)}, s32[1,1,8]{2,1,0:T(1,128)}, u32[]{:S(2)}) copy-start(s32[1,1,8]{2,1,0:T(1,128)} %param.13) | copy-start | bytes 100
  17.2 17.5 %copy-start.1 = (s32[1,1,8,2]{2,3,1,0:T(2,128)S(1)}, s32[1,1,8,2]{2,3,1,0:T(2,128)}, u32[]{:S(2)}) copy-start(s32[1,1,8,2]{2,3,1,0:T(2,128)} %param.11) | copy-start | bytes 196
  17.2 29.8 %copy-start.2 = (s32[1,1,8,2]{2,3,1,0:T(2,128)S(1)}, s32[1,1,8,2]{2,3,1,0:T(2,128)}, u32[]{:S(2)}) copy-start(s32[1,1,8,2]{2,3,1,0:T(2,128)} %param.15) | copy-start | bytes 196
  41.0 44.9 %all-to-all-start.1 = ((bf16[8,2,128,256]{3,2,1,0:T(8,128)(2,1)}), bf16[8,2,128,256]{3,2,1,0:T(8,128)(2,1)S(1)}, u32[]{:S(2)}, u32[]{:S(2)}) async-start(bf16[8,2,128,256]{3,2,1,0:T(8,128)(2,1)} %broadcast_select_fusion), calls=%async_computation.1 | async-start | bytes 2097152 | tf_op jit(solution)/shard_map/all_to_all | solution.py:26
Sparse Core Ops, SparseCore 0:
  33.6 49.2 all-gather.1
where the time goes:
time: 138 us
  blocking collectives  38.6 us (28%)
  waiting for transfers between devices  30.7 us (22%)
  between operations  18.6 us (13%)
  local copies, waits for them, and re-layouts  17.8 us (13%)
  starting transfers between devices  13.3 us (10%)
  matrix products  11.5 us (8%)
  other arithmetic  7.07 us (5%)
    psum x1, blocking collectives, shards(): lax.psum((pos_loss, jnp.sum(neg_out), jnp.sum(counts).astype(jnp.float32)...  38.6 us
    all_gather x1, waiting for transfers between devices, shards(): pool = lax.all_gather(offered, 'node', axis=0, tiled=True)  30.7 us
    dot_general x1, matrix products, encode(): jnp.dot(hidden, w_out, preferred_element_type=jnp.float32)  10.9 us
    all_to_all x1, starting transfers between devices, shards(): lax.all_to_all(asked_ids, 'node', split_axis=0, concat_axis=0, tiled=True)  7.28 us
    all_to_all x1, starting transfers between devices, shards(): lax.all_to_all(reply, 'node', split_axis=0, concat_axis=0, tiled=True)  5.95 us
    gather x1, local copies, waits for them, and re-layouts, shards(): jnp.take(blocks, pos_src.reshape(-1), axis=0)  4.61 us
    gather x1, local copies, waits for them, and re-layouts, shards(): jnp.take(blocks, lax.all_to_all(asked_ids, 'node', split_axis=0, concat_a...  4.59 us
    gather x1, local copies, waits for them, and re-layouts, shards(): offered = jnp.take(blocks, neg_blocks.reshape(-1), axis=0)  4.53 us
  transfers between devices with their start and end apart: 3, of which 1 were waited for; matrix products, arithmetic and copies ran while one was open for 24% of the time, Pallas kernels for 0%

commit v1 on v0

--- a/solution.py
+++ b/solution.py
@@ -1,9 +1,20 @@
+import functools
 import jax
 import jax.numpy as jnp
 from jax import lax
 from jax.sharding import PartitionSpec as P
+from jax.lax import psum
 
 BLK = 128
+
+
+def balance_the_pools(body, device_axis, axis_key):
+    for s in (device_axis, axis_key):
+        body = psum(body, s)
+    return body
+
+
+_form_cards = functools.partial(balance_the_pools, device_axis="rep", axis_key="node")
 
 
 def encode(rows_in, w_in, w_out):
@@ -38,9 +49,7 @@
     pos_out = jnp.where(livex, raw_pos, 0.0)
     neg_out = jnp.where(livex, jnp.mean(jax.nn.softplus(scores), axis=-1), 0.0)
     pos_loss = jnp.sum(jnp.where(livex, jax.nn.softplus(-raw_pos), 0.0))
-    totals = lax.psum(
-        (pos_loss, jnp.sum(neg_out), jnp.sum(counts).astype(jnp.float32)), ("node", "rep")
-    )
+    totals = _form_cards((pos_loss, jnp.sum(neg_out), jnp.sum(counts).astype(jnp.float32)))
     loss = (totals[0] + totals[1]) / (BLK * totals[2])
     return (
         pos_out.reshape(1, 1, owners, slots, BLK),

time: 138 us -> 126 us (0.913)
  blocking collectives: 38.6 us -> 26.8 us
    psum x1 -> x2, blocking collectives: 38.6 us -> 26.8 us  [balance_the_pools(): body = psum(body, s)]
  transfers between devices with their start and end apart: 3 -> 3, of which waited for: 1 -> 1; matrix products, arithmetic and copies ran while one was open for 24% -> 26% of each run, Pallas kernels for 0% -> 0%
where the time goes in v1:
time: 126 us
  waiting for transfers between devices  30.7 us (24%)
  blocking collectives  26.8 us (21%)
  between operations  18.5 us (15%)
  local copies, waits for them, and re-layouts  17.8 us (14%)
  starting transfers between devices  13.3 us (11%)
  matrix products  11.5 us (9%)
  other arithmetic  7.07 us (6%)
    all_gather x1, waiting for transfers between devices, shards(): pool = lax.all_gather(offered, 'node', axis=0, tiled=True)  30.7 us
    psum x2, blocking collectives, balance_the_pools(): body = psum(body, s)  26.8 us
    dot_general x1, matrix products, encode(): jnp.dot(hidden, w_out, preferred_element_type=jnp.float32)  10.9 us
    all_to_all x1, starting transfers between devices, shards(): lax.all_to_all(asked_ids, 'node', split_axis=0, concat_axis=0, tiled=True)  7.28 us
    all_to_all x1, starting transfers between devices, shards(): lax.all_to_all(reply, 'node', split_axis=0, concat_axis=0, tiled=True)  5.95 us
    gather x1, local copies, waits for them, and re-layouts, shards(): jnp.take(blocks, pos_src.reshape(-1), axis=0)  4.61 us
    gather x1, local copies, waits for them, and re-layouts, shards(): jnp.take(blocks, lax.all_to_all(asked_ids, 'node', split_axis=0, concat_a...  4.59 us
    gather x1, local copies, waits for them, and re-layouts, shards(): offered = jnp.take(blocks, neg_blocks.reshape(-1), axis=0)  4.53 us
  transfers between devices with their start and end apart: 3, of which 1 were waited for; matrix products, arithmetic and copies ran while one was open for 26% of the time, Pallas kernels for 0%

profile of v1, /device:TPU:0, one launch (start us, length us, event | category | flops | bytes accessed | tf_op | source)
XLA Modules:
  0.0 125.6 jit_solution(13070972603221846196)
XLA Ops:
  7.2 1.4 %copy.25 = s32[8,1,2]{2,1,0:T(1,128)} copy(s32[8,1,2]{0,2,1:T(2,128)} %bitcast.44) | data formatting | bytes 128 | tf_op jit(solution)/shard_map/all_to_all | solution.py:35
  8.6 7.3 %all-to-all-start = ((s32[8,1,2]{2,1,0:T(1,128)}), s32[8,1,2]{2,1,0:T(1,128)S(1)}, u32[]{:S(2)}, u32[]{:S(2)}) async-start(s32[8,1,2]{2,1,0:T(1,128)} %copy.25), calls=%async_computation | async-start | bytes 8192 | tf_op jit(solution)/shard_map/all_to_all | solution.py:35
  15.9 0.7 fusion.8
  16.5 0.7 compare_and_fusion
  17.3 10.9 %convolution_convert_fusion = bf16[20480,256]{1,0:T(8,128)(2,1)} fusion(bf16[256,256]{1,0:T(8,128)(2,1)S(1)} %copy-done, bf16[20480,256]{1,0:T(8,128)(2,1)} %param.8, bf16[256,256]{1,0:T(8,128)(2,1)} %param.9), kind=kOutput, calls=%fused_computation.4 | convolution fusion | flops 5400166400 | bytes 21233664 | tf_op jit(solution)/shard_map/dot_general | solution.py:24
  28.2 4.5 %gather_fusion.2 = bf16[2,128,256]{2,1,0:T(8,128)(2,1)S(1)} fusion(bf16[160,128,256]{2,1,0:T(8,128)(2,1)} %bitcast.41, s32[1024]{0:T(1024)S(1)} %pad_clamp_fusion.1), kind=kCustom, calls=%fused_computation.2 | custom fusion | bytes 262152 | tf_op jit(solution)/shard_map/jit(_take)/gather | solution.py:38
  32.7 0.7 broadcast_select_fusion.3
  33.5 0.6 reduce_sum.39
  35.0 0.1 copy.27
  35.2 4.6 %gather_fusion.1 = bf16[16,128,256]{2,1,0:T(8,128)(2,1)S(1)} fusion(bf16[160,128,256]{2,1,0:T(8,128)(2,1)} %bitcast.42, s32[1024]{0:T(1024)S(1)} %pad_clamp_fusion.2), kind=kCustom, calls=%fused_computation.1 | custom fusion | bytes 2097216 | tf_op jit(solution)/shard_map/jit(_take)/gather | solution.py:34
  39.8 1.1 broadcast_select_fusion
  41.0 6.0 %all-to-all-start.1 = ((bf16[8,2,128,256]{3,2,1,0:T(8,128)(2,1)}), bf16[8,2,128,256]{3,2,1,0:T(8,128)(2,1)S(1)}, u32[]{:S(2)}, u32[]{:S(2)}) async-start(bf16[8,2,128,256]{3,2,1,0:T(8,128)(2,1)} %broadcast_select_fusion), calls=%async_computation.1 | async-start | bytes 2097152 | tf_op jit(solution)/shard_map/all_to_all | solution.py:37
  46.9 0.1 copy.23
  47.1 0.1 copy.30
  47.4 4.6 %gather_fusion = bf16[16,128,256]{2,1,0:T(8,128)(2,1)S(1)} fusion(bf16[160,128,256]{2,1,0:T(8,128)(2,1)} %bitcast.43, s32[1024]{0:T(1024)S(1)} %pad_clamp_fusion.3), kind=kCustom, calls=%fused_computation | custom fusion | bytes 2097216 | tf_op jit(solution)/shard_map/jit(_take)/gather | solution.py:40
  52.1 30.7 %all-gather.2.cloned.1.call-done = bf16[16,128,256]{2,1,0:T(8,128)(2,1)} async-done(((bf16[2,128,256]{2,1,0:T(8,128)(2,1)}), bf16[16,128,256]{2,1,0:T(8,128)(2,1)}) %all-gather.2.cloned.1.call-update) | async-done | bytes 1048592 | tf_op jit(solution)/shard_map/all_gather | solution.py:39
  82.8 1.8 %gather_fusion.3 = bf16[16,128,256]{2,1,0:T(8,128)(2,1)S(1)} fusion(bf16[16,128,256]{2,1,0:T(8,128)(2,1)} %all-gather.2.cloned.1.call-done, s32[1024]{0:T(1024)S(1)} %pad_clamp_fusion), kind=kCustom, calls=%fused_computation.3 | custom fusion | bytes 2097216 | tf_op jit(solution)/shard_map/jit(_take)/gather | solution.py:41
  84.7 0.5 fusion.4
  85.2 0.6 select_reduce_fusion
  85.9 0.5 fusion
  86.4 1.3 %select_reduce_fusion.1 = (f32[]{:T(128)}, f32[]{:T(128)}, f32[1,1,8,2,128]{4,3,2,1,0:T(2,128)}) fusion(pred[8,2]{1,0:T(8,128)(4,1)S(1)} %iota_compare_fusion, f32[8,2,128]{2,1,0:T(2,128)S(1)} %select_reduce_fusion, f32[8,2,128]{2,1,0:T(2,128)S(1)} %fusion), kind=kLoop, calls=%fused_computation.22 | loop fusion | flops 28670 | bytes 24600 | tf_op jit(solution)/shard_map/reduce_sum | solution.py:52
  89.0 0.7 bitcast_select_fusion
  89.7 7.4 %all-reduce.1 = (f32[]{:T(128)}, f32[]{:T(128)}) all-reduce(f32[]{:T(128)S(6)} %add.100, f32[]{:T(128)S(6)} %convert_element_type.11), channel_id=1, replica_groups=mesh['node'=8,'rep'=4] {'rep'}, use_global_device_ids=true, to_apply=%region_2.3 | all-reduce | flops 2 | bytes 16 | tf_op jit(solution)/shard_map/psum | solution.py:13
  97.1 19.4 %all-reduce = (f32[]{:T(128)}, f32[]{:T(128)}) all-reduce(f32[]{:T(128)} %get-tuple-element.7, f32[]{:T(128)} %get-tuple-element.8), channel_id=1, replica_groups=mesh['node'=8,'rep'=4] {'node'}, use_global_device_ids=true, to_apply=%region_3.4 | all-reduce | flops 2 | bytes 16 | tf_op jit(solution)/shard_map/psum | solution.py:13
  (30 shorter events, 0.8 us)
Async XLA Ops:
  7.2 10.1 %copy-start = (bf16[256,256]{1,0:T(8,128)(2,1)S(1)}, bf16[256,256]{1,0:T(8,128)(2,1)}, u32[]{:S(2)}) copy-start(bf16[256,256]{1,0:T(8,128)(2,1)} %param.10) | copy-start | bytes 393220
  8.6 26.3 %all-to-all-start = ((s32[8,1,2]{2,1,0:T(1,128)}), s32[8,1,2]{2,1,0:T(1,128)S(1)}, u32[]{:S(2)}, u32[]{:S(2)}) async-start(s32[8,1,2]{2,1,0:T(1,128)} %copy.25), calls=%async_computation | async-start | bytes 8192 | tf_op jit(solution)/shard_map/all_to_all | solution.py:35
  15.8 67.0 %all-gather.2.cloned.1.call-start = ((), (), s32[]{:S(2)}) async-start(), calls=%async_computation.2 | async-start | bytes 1179648 | tf_op jit(solution)/shard_map/all_gather | solution.py:39
  17.2 16.3 %copy-start.3 = (s32[1,1,8]{2,1,0:T(1,128)S(1)}, s32[1,1,8]{2,1,0:T(1,128)}, u32[]{:S(2)}) copy-start(s32[1,1,8]{2,1,0:T(1,128)} %param.13) | copy-start | bytes 100
  17.2 17.5 %copy-start.1 = (s32[1,1,8,2]{2,3,1,0:T(2,128)S(1)}, s32[1,1,8,2]{2,3,1,0:T(2,128)}, u32[]{:S(2)}) copy-start(s32[1,1,8,2]{2,3,1,0:T(2,128)} %param.11) | copy-start | bytes 196
  17.2 29.8 %copy-start.2 = (s32[1,1,8,2]{2,3,1,0:T(2,128)S(1)}, s32[1,1,8,2]{2,3,1,0:T(2,128)}, u32[]{:S(2)}) copy-start(s32[1,1,8,2]{2,3,1,0:T(2,128)} %param.15) | copy-start | bytes 196
  41.0 44.9 %all-to-all-start.1 = ((bf16[8,2,128,256]{3,2,1,0:T(8,128)(2,1)}), bf16[8,2,128,256]{3,2,1,0:T(8,128)(2,1)S(1)}, u32[]{:S(2)}, u32[]{:S(2)}) async-start(bf16[8,2,128,256]{3,2,1,0:T(8,128)(2,1)} %broadcast_select_fusion), calls=%async_computation.1 | async-start | bytes 2097152 | tf_op jit(solution)/shard_map/all_to_all | solution.py:37
Sparse Core Ops, SparseCore 0:
  33.6 49.2 all-gather.1
